TPU v7x, 32 devices: a whole 2x2x4 slice. The times are simulated.
32 devices in a mesh: wide: 16 (over z, y, x), narrow: 2 (over core).
Axes of the slice: x: 2, y: 2, z: 4, core: 2. Of those that a mesh axis runs over, the one named last changes fastest.
Arguments:
- features: bfloat16 [512, 16384], P('wide', 'narrow'), may hold values from -6 to 6
- queries: bfloat16 [1024, 16384], P('wide', 'narrow'), may hold values from -6 to 6
- damping: float32 [16384], P('wide'), may hold values from 0.25 to 4
Outputs:
- kernel: float32 [16384, 16384], P('wide', 'narrow')
- factor: float32 [16384, 256], P('wide')
- scores: float32 [1024, 512], P('wide', 'narrow')
All inputs are finite; a program needn't handle non-finite values.
Results may differ from a plain program's by a relative error of at most 0.0003.
Values may be sent and summed in bfloat16 or wider, within the bound.
No kernel may reach another device: no remote copies, remote signals or barrier semaphores. Data moves between devices by JAX's collectives and lax.ppermute only.
A program may use at most 128 MiB of HBM per device.

v0:
```python
import math
import jax
import jax.numpy as jnp
from jax import lax
from jax.sharding import PartitionSpec as P

P_SIZE = 16384
PANEL = 128
PANELS = 2


def broadcast(x, axis, root):
    mine = lax.axis_index(axis) == root
    return lax.psum(jnp.where(mine, x, jnp.zeros_like(x)), axis)


def on_device(features, queries, damping):
    rows_here = damping.shape[0]
    cols_here = queries.shape[1]
    slab_total = features.shape[0] * lax.axis_size("wide")
    wide_pos = lax.axis_index("wide")
    narrow_pos = lax.axis_index("narrow")
    contract_rows = (((0,), (0,)), ((), ()))
    contract_cols = (((1,), (1,)), ((), ()))
    full_width = lax.all_gather(features, "narrow", axis=1, tiled=True)
    row_features = lax.all_to_all(full_width, "wide", split_axis=1, concat_axis=0, tiled=True)
    slab_columns = lax.all_gather(features, "wide", axis=0, tiled=True)
    products = lax.dot_general(
        row_features, slab_columns, contract_rows, preferred_element_type=jnp.float32
    )
    partial_value = lax.dot_general(
        queries, slab_columns, contract_cols, preferred_element_type=jnp.float32
    )
    scores = lax.psum_scatter(partial_value, "narrow", scatter_dimension=1, tiled=True) * (
        1.0 / math.sqrt(P_SIZE)
    )
    row_ids = wide_pos * rows_here + lax.broadcasted_iota(jnp.int32, (rows_here, 1), 0)
    col_ids = narrow_pos * cols_here + lax.broadcasted_iota(jnp.int32, (1, cols_here), 1)
    kernel_block = products / slab_total + jnp.where(
        row_ids == col_ids, damping[:, None], jnp.float32(0.0)
    )
    factors = []
    for panel_index in range(PANELS):
        offset = panel_index * PANEL
        column_root = offset // cols_here
        row_root = offset // rows_here
        col_shift = offset % cols_here
        row_shift = offset % rows_here
        panel_columns = broadcast(
            kernel_block[:, col_shift : col_shift + PANEL], "narrow", column_root
        )
        pivot_block = broadcast(panel_columns[row_shift : row_shift + PANEL], "wide", row_root)
        pivot_factor = jnp.linalg.cholesky(pivot_block)
        lower_rows = lax.linalg.triangular_solve(
            pivot_factor, panel_columns, left_side=False, lower=True, transpose_a=True
        )
        pivot_rows = broadcast(kernel_block[row_shift : row_shift + PANEL], "wide", row_root)
        lower_cols = lax.linalg.triangular_solve(
            pivot_factor, pivot_rows, left_side=True, lower=True, transpose_a=False
        ).T
        kernel_block = kernel_block - jnp.dot(
            lower_rows,
            lower_cols.T,
            precision=lax.Precision.HIGHEST,
            preferred_element_type=jnp.float32,
        )
        boundary = offset + PANEL
        kernel_block = jnp.where(
            (row_ids < boundary) | (col_ids < boundary), jnp.zeros_like(kernel_block), kernel_block
        )
        factors.append(lower_rows)
    return (kernel_block, jnp.concatenate(factors, axis=1), scores)


def solution(mesh):
    return jax.shard_map(
        on_device,
        mesh=mesh,
        in_specs=(P("wide", "narrow"), P("wide", "narrow"), P("wide")),
        out_specs=(P("wide", "narrow"), P("wide", None), P("wide", "narrow")),
        check_vma=False,
    )
```

profile of v0, /device:TPU:0, one launch (start us, length us, event | category | flops | bytes accessed | tf_op | source)
XLA Modules:
  0.0 752.9 jit_solution(7625984602944274443)
XLA Ops:
  7.2 0.0 copy-start
  7.2 0.0 all-gather.3.cloned.1.call-start
  7.2 0.7 all-gather.3.cloned.1.call-update
  7.9 0.0 all-gather.5.cloned.1.call-start
  8.0 0.7 all-gather.5.cloned.1.call-update
  8.7 12.7 %all-gather.3.cloned.1.call-done = bf16[32,16384]{1,0:T(8,128)(2,1)} async-done(((bf16[32,8192]{1,0:T(8,128)(2,1)}), bf16[32,16384]{1,0:T(8,128)(2,1)}) %all-gather.3.cloned.1.call-update) | async-done | bytes 1048592 | tf_op jit(solution)/shard_map/all_gather | solution.py:25
  21.3 2.3 copy.41
  23.6 6.8 all-to-all-start
  30.4 0.0 all-reduce.7.cloned.1.call-start
  30.5 35.8 %all-to-all-done = bf16[32,16,1024]{2,0,1:T(8,128)(2,1)S(1)} async-done(((bf16[32,16,1024]{2,0,1:T(8,128)(2,1)}), bf16[32,16,1024]{2,0,1:T(8,128)(2,1)S(1)}, u32[]{:S(2)}, u32[]{:S(2)}) %all-to-all-start) | async-done | bytes 1048608 | tf_op jit(solution)/shard_map/all_to_all | solution.py:26
  66.3 85.7 %all-gather.5.cloned.1.call-done = bf16[512,8192]{1,0:T(8,128)(2,1)} async-done(((bf16[32,8192]{1,0:T(8,128)(2,1)}), bf16[512,8192]{1,0:T(8,128)(2,1)}) %all-gather.5.cloned.1.call-update) | async-done | bytes 8388624 | tf_op jit(solution)/shard_map/all_gather | solution.py:27
  151.9 19.3 %select_add_fusion = f32[1024,8192]{0,1:T(8,128)} fusion(bf16[512,1024]{1,0:T(8,128)(2,1)S(1)} %bitcast.49, bf16[512,8192]{1,0:T(8,128)(2,1)} %all-gather.5.cloned.1.call-done, f32[1024]{0:T(1024)} %param.10, s32[1024]{0:T(1024)S(1)} %iota_add_fusion.1, s32[8192]{0:T(1024)S(1)} %iota_add_fusion), kind=kOutput, calls=%fused_computation.2 | convolution fusion | flops 8623489024 | bytes 43032576 | tf_op jit(solution)/shard_map/dot_general | solution.py:28
  171.3 1.9 slice_select_fusion.3
  173.2 0.0 all-reduce.7.cloned.1.call-update
  173.2 0.0 all-reduce.13.cloned.1.call-start
  173.2 4.4 slice_select_fusion.1
  177.6 12.5 %all-reduce.7.cloned.1.call-done = f32[1024,128]{0,1:T(8,128)} async-done(((f32[1024,128]{0,1:T(8,128)}), f32[1024,128]{0,1:T(8,128)}) %all-reduce.7.cloned.1.call-update) | async-done | bytes 524304 | tf_op jit(solution)/shard_map/psum | solution.py:14
  190.1 0.0 copy-start.3
  190.1 1.5 slice_select_fusion.5
  191.7 0.0 all-reduce.13.cloned.1.call-update
  191.7 0.3 all-reduce.9.cloned.1.call-start
  192.1 175.9 %all-reduce.13.cloned.1.call-done = (f32[128,128]{0,1:T(8,128)}, f32[128,8192]{0,1:T(8,128)}) async-done(((f32[128,128]{0,1:T(8,128)}, f32[128,8192]{0,1:T(8,128)}), (f32[128,128]{0,1:T(8,128)}, f32[128,8192]{0,1:T(8,128)})) %all-reduce.13.cloned.1.call-update) | async-done | bytes 4259856 | tf_op jit(solution)/shard_map/psum | solution.py:14
  368.0 0.9 copy.30
  368.9 0.9 fusion.9
  369.7 11.7 %cholesky.44 = f32[128,128]{1,0:T(8,128)S(1)} custom-call(f32[128,128]{1,0:T(8,128)S(1)} %fusion.9), custom_call_target="Cholesky" | custom-call | tf_op jit(solution)/shard_map/jit(cholesky)/cholesky | solution.py:53
  381.5 0.6 compare_reduce_fusion.1
  382.1 0.7 fusion
  382.8 9.8 %custom-call.10 = f32[1,128,128]{1,2,0:T(8,128)S(1)} custom-call(f32[1,128,128]{2,1,0:T(8,128)S(1)} %fusion), custom_call_target="InvertDiagBlocksLowerTriangular" | custom-call | tf_op jit(solution)/shard_map/triangular_solve/custom-call.0 | solution.py:54
  392.6 6.1 fusion.6
  398.7 0.0 copy-done.3
  398.7 0.6 convolution_bitcast_fusion.1
  399.3 35.1 %subtract_select_fusion.1 = f32[1024,8192]{0,1:T(8,128)} fusion(f32[1024,8192]{0,1:T(8,128)} %select_add_fusion, f32[1024,128]{0,1:T(8,128)S(1)} %convolution_bitcast_fusion.1, f32[128,8192]{1,0:T(8,128)S(1)} %fusion.6, pred[1024]{0:T(1024)(128)(4,1)S(1)} %fusion.12, pred[8192]{0:T(1024)(128)(4,1)S(1)} %fusion.10), kind=kOutput, calls=%fused_computation.1 | convolution fusion | flops 12910067712 | bytes 71836672 | tf_op jit(solution)/shard_map/dot_general | solution.py:61
  434.5 1.9 slice_select_fusion.2
  436.4 0.0 all-reduce.9.cloned.1.call-update
  436.4 0.0 reduce-scatter.2.cloned.1.call-start
  436.4 0.0 copy-done
  436.4 6.7 fusion.14
  443.1 0.0 reduce-scatter.2.cloned.1.call-update
  443.2 0.2 all-reduce.11.cloned.1.call-start
  443.4 4.4 slice_select_fusion
  447.8 6.4 all-reduce.9.cloned.1.call-done
  454.2 0.0 copy-start.2
  454.2 1.5 slice_select_fusion.4
  455.7 0.0 all-reduce.11.cloned.1.call-update
  455.8 9.3 %reduce-scatter.2.cloned.1.call-done = f32[64,256]{1,0:T(8,128)} async-done(((f32[64,512]{1,0:T(8,128)}), f32[64,256]{1,0:T(8,128)}) %reduce-scatter.2.cloned.1.call-update) | async-done | bytes 65552 | tf_op jit(solution)/shard_map/reduce_scatter | solution.py:34
  465.1 1.5 broadcast_multiply_fusion
  466.5 176.4 %all-reduce.11.cloned.1.call-done = (f32[128,128]{0,1:T(8,128)}, f32[128,8192]{0,1:T(8,128)}) async-done(((f32[128,128]{0,1:T(8,128)}, f32[128,8192]{0,1:T(8,128)}), (f32[128,128]{0,1:T(8,128)}, f32[128,8192]{0,1:T(8,128)})) %all-reduce.11.cloned.1.call-update) | async-done | bytes 4259856 | tf_op jit(solution)/shard_map/psum | solution.py:14
  643.0 0.9 copy.32
  643.9 0.9 fusion.5
  644.7 11.7 %cholesky.55 = f32[128,128]{1,0:T(8,128)S(1)} custom-call(f32[128,128]{1,0:T(8,128)S(1)} %fusion.5), custom_call_target="Cholesky" | custom-call | tf_op jit(solution)/shard_map/jit(cholesky)/cholesky | solution.py:53
  656.5 0.6 compare_reduce_fusion
  657.1 0.7 fusion.1
  657.8 9.8 %custom-call.12 = f32[1,128,128]{1,2,0:T(8,128)S(1)} custom-call(f32[1,128,128]{2,1,0:T(8,128)S(1)} %fusion.1), custom_call_target="InvertDiagBlocksLowerTriangular" | custom-call | tf_op jit(solution)/shard_map/triangular_solve/custom-call.0 | solution.py:54
  667.6 8.0 %fusion.2 = f32[128,8192]{1,0:T(8,128)} fusion(f32[128,8192]{0,1:T(8,128)} %get-tuple-element.19, f32[1,128,128]{1,2,0:T(8,128)S(1)} %custom-call.12), kind=kOutput, calls=%fused_computation.17 | convolution fusion | flops 1610612736 | bytes 8454144 | tf_op jit(solution)/shard_map/triangular_solve/dot.0 | solution.py:58
  675.6 0.0 copy-done.2
  675.6 0.6 convolution_bitcast_fusion
  676.3 0.1 pad_maximum_fusion
  676.3 1.3 copy.35
  677.7 37.0 %subtract_select_fusion = f32[1024,8192]{0,1:T(8,128)} fusion(f32[1024,8192]{0,1:T(8,128)} %subtract_select_fusion.1, f32[1024,128]{0,1:T(8,128)S(1)} %convolution_bitcast_fusion, f32[128,8192]{1,0:T(8,128)} %fusion.2, pred[1024]{0:T(1024)(128)(4,1)S(1)} %fusion.13, pred[8192]{0:T(1024)(128)(4,1)S(1)} %fusion.11), kind=kOutput, calls=%fused_computation | convolution fusion | flops 12910067712 | bytes 71836672 | tf_op jit(solution)/shard_map/dot_general | solution.py:61
  714.6 0.0 copy-start.1
  714.6 31.2 %copy.34 = f32[1024,8192]{1,0:T(8,128)} copy(f32[1024,8192]{0,1:T(8,128)} %subtract_select_fusion) | data formatting | bytes 67108864
  745.8 0.0 copy-done.1
  (8 shorter events, 0.1 us)
Async XLA Ops:
  7.2 429.3 %copy-start = (bf16[64,8192]{1,0:T(8,128)(2,1)S(1)}, bf16[64,8192]{1,0:T(8,128)(2,1)}, u32[]{:S(2)}) copy-start(bf16[64,8192]{1,0:T(8,128)(2,1)} %param.9) | copy-start | bytes 3145732
  7.2 14.1 %all-gather.3.cloned.1.call-start = ((), (), s32[]{:S(2)}) async-start(), calls=%async_computation.2 | async-start | bytes 1572864 | tf_op jit(solution)/shard_map/all_gather | solution.py:25
  7.9 144.0 %all-gather.5.cloned.1.call-start = ((), (), s32[]{:S(2)}) async-start(), calls=%async_computation.3 | async-start | bytes 8912896 | tf_op jit(solution)/shard_map/all_gather | solution.py:27
  23.6 42.7 %all-to-all-start = ((bf16[32,16,1024]{2,0,1:T(8,128)(2,1)}), bf16[32,16,1024]{2,0,1:T(8,128)(2,1)S(1)}, u32[]{:S(2)}, u32[]{:S(2)}) async-start(bf16[32,16,1024]{2,0,1:T(8,128)(2,1)} %bitcast.48), calls=%async_computation | async-start | bytes 2097152 | tf_op jit(solution)/shard_map/all_to_all | solution.py:26
  30.4 159.7 %all-reduce.7.cloned.1.call-start = ((), (), s32[]{:S(2)}) async-start(), calls=%async_computation.4 | async-start | bytes 1048576 | tf_op jit(solution)/shard_map/psum | solution.py:14
  173.2 194.8 %all-reduce.13.cloned.1.call-start = ((), (), s32[]{:S(2)}) async-start(), calls=%async_computation.8 | async-start | bytes 8519680 | tf_op jit(solution)/shard_map/psum | solution.py:14
  190.1 208.6 %copy-start.3 = (f32[1024,128]{0,1:T(8,128)S(1)}, f32[1024,128]{0,1:T(8,128)}, u32[]{:S(2)}) copy-start(f32[1024,128]{0,1:T(8,128)} %all-reduce.7.cloned.1.call-done) | copy-start | bytes 1572868
  191.7 262.5 %all-reduce.9.cloned.1.call-start = ((), (), s32[]{:S(2)}) async-start(), calls=%async_computation.5 | async-start | bytes 1048576 | tf_op jit(solution)/shard_map/psum | solution.py:14
  436.4 28.7 %reduce-scatter.2.cloned.1.call-start = ((), (), s32[]{:S(2)}) async-start(), calls=%async_computation.6 | async-start | bytes 196608 | tf_op jit(solution)/shard_map/reduce_scatter | solution.py:34
  443.2 199.8 %all-reduce.11.cloned.1.call-start = ((), (), s32[]{:S(2)}) async-start(), calls=%async_computation.7 | async-start | bytes 8519680 | tf_op jit(solution)/shard_map/psum | solution.py:14
  454.2 221.4 %copy-start.2 = (f32[1024,128]{0,1:T(8,128)S(1)}, f32[1024,128]{0,1:T(8,128)}, u32[]{:S(2)}) copy-start(f32[1024,128]{0,1:T(8,128)} %all-reduce.9.cloned.1.call-done) | copy-start | bytes 1572868
  714.6 31.2 %copy-start.1 = (bf16[64,8192]{1,0:T(8,128)(2,1)S(1)}, bf16[64,8192]{1,0:T(8,128)(2,1)}, u32[]{:S(2)}) copy-start(bf16[64,8192]{1,0:T(8,128)(2,1)} %param.9) | copy-start | bytes 3145732
Sparse Core Ops, SparseCore 0:
  9.5 11.7 all-gather.2
  24.1 127.8 all-gather.4
  173.3 16.7 all-reduce.6
  196.5 171.4 all-reduce.12
  436.5 17.6 all-reduce.8
  456.2 8.7 reduce-scatter.1
  471.6 171.3 all-reduce.10
where the time goes:
time: 759 us; the launch traced here: 753 us
  waiting for transfers between devices  516 us (68%)
  matrix products  113 us (15%)
  other arithmetic  64.7 us (9%)
  local copies, waits for them, and re-layouts  36.6 us (5%)
  between operations  14.5 us (2%)
    psum x4, waiting for transfers between devices, broadcast(): return lax.psum(jnp.where(mine, x, jnp.zeros_like(x)), axis)  371 us
    all_gather x1, waiting for transfers between devices, on_device(): slab_columns = lax.all_gather(features, 'wide', axis=0, tiled=True)  85.7 us
    dot_general x2, matrix products, on_device(): jnp.dot(lower_rows, lower_cols.T, precision=lax.Precision.HIGHEST, prefer...  72.1 us
    all_to_all x1, waiting for transfers between devices, on_device(): lax.all_to_all(full_width, 'wide', split_axis=1, concat_axis=0, tiled=True)  35.8 us
    unnamed x10, local copies, waits for them, and re-layouts  32.5 us
    another operation x6, other arithmetic, on_device(): pivot_factor = jnp.linalg.cholesky(pivot_block)  24.8 us
    another operation x4, other arithmetic, on_device(): lax.linalg.triangular_solve(pivot_factor, panel_columns, left_side=False,...  20.9 us
    dot_general x1, matrix products, on_device(): lax.dot_general(row_features, slab_columns, contract_rows, preferred_elem...  19.3 us
  transfers between devices with their start and end apart: 8, of which 8 were waited for; matrix products, arithmetic and copies ran while one was open for 3% of the time, Pallas kernels for 0%

commit v1 on v0

--- a/solution.py
+++ b/solution.py
@@ -11,7 +11,7 @@
 
 def broadcast(x, axis, root):
     mine = lax.axis_index(axis) == root
-    return lax.psum(jnp.where(mine, x, jnp.zeros_like(x)), axis)
+    return jnp.sum(lax.all_gather(jnp.where(mine, x, jnp.zeros_like(x)), axis), axis=0)
 
 
 def on_device(features, queries, damping):

time: 759 us -> 1800 us (2.37)
  waiting for transfers between devices: 516 us -> 1550 us
  other arithmetic: 64.7 us -> 113 us
  local copies, waits for them, and re-layouts: 36.6 us -> 3.79 us
    all_gather x0 -> x6, waiting for transfers between devices: none -> 1410 us  [broadcast(): lax.all_gather(jnp.where(mine, x, jnp.zeros_like(x)), axis)]
    psum x4 -> x0, waiting for transfers between devices: 371 us -> none  [broadcast(): return lax.psum(jnp.where(mine, x, jnp.zeros_like(x)), axis)]
    reduce_sum x0 -> x6, other arithmetic: none -> 51.7 us  [broadcast(): jnp.sum(lax.all_gather(jnp.where(mine, x, jnp.zeros_like(x)), axis), axis=0)]
    unnamed x10 -> x5, local copies, waits for them, and re-layouts: 32.5 us -> 1.33 us
  transfers between devices with their start and end apart: 8 -> 10, of which waited for: 8 -> 10; matrix products, arithmetic and copies ran while one was open for 3% -> 4% of each run, Pallas kernels for 0% -> 0%
where the time goes in v1:
time: 1800 us
  waiting for transfers between devices  1550 us (86%)
  other arithmetic  113 us (6%)
  matrix products  110 us (6%)
    all_gather x6, waiting for transfers between devices, broadcast(): lax.all_gather(jnp.where(mine, x, jnp.zeros_like(x)), axis)  1410 us
    all_gather x1, waiting for transfers between devices, on_device(): slab_columns = lax.all_gather(features, 'wide', axis=0, tiled=True)  85.7 us
    dot_general x2, matrix products, on_device(): jnp.dot(lower_rows, lower_cols.T, precision=lax.Precision.HIGHEST, prefer...  69.8 us
    reduce_sum x6, other arithmetic, broadcast(): jnp.sum(lax.all_gather(jnp.where(mine, x, jnp.zeros_like(x)), axis), axis=0)  51.7 us
  transfers between devices with their start and end apart: 10, of which 10 were waited for; matrix products, arithmetic and copies ran while one was open for 4% of the time, Pallas kernels for 0%

profile of v1, /device:TPU:0, one launch (start us, length us, event | category | flops | bytes accessed | tf_op | source)
XLA Modules:
  0.0 1795.4 jit_solution(9908659970879852203)
XLA Ops:
  7.2 0.0 copy-start
  7.2 0.0 all-gather.15.cloned.1.call-start
  7.2 0.7 all-gather.15.cloned.1.call-update
  7.9 0.0 all-gather.17.cloned.1.call-start
  8.0 0.7 all-gather.17.cloned.1.call-update
  8.7 12.7 all-gather.15.cloned.1.call-done
  21.3 2.3 copy.26
  23.6 6.8 all-to-all-start
  30.4 0.0 all-gather.19.cloned.1.call-start
  30.5 35.8 %all-to-all-done = bf16[32,16,1024]{2,0,1:T(8,128)(2,1)S(1)} async-done(((bf16[32,16,1024]{2,0,1:T(8,128)(2,1)}), bf16[32,16,1024]{2,0,1:T(8,128)(2,1)S(1)}, u32[]{:S(2)}, u32[]{:S(2)}) %all-to-all-start) | async-done | bytes 1048608 | tf_op jit(solution)/shard_map/all_to_all | solution.py:26
  66.3 85.7 %all-gather.17.cloned.1.call-done = bf16[512,8192]{1,0:T(8,128)(2,1)} async-done(((bf16[32,8192]{1,0:T(8,128)(2,1)}), bf16[512,8192]{1,0:T(8,128)(2,1)}) %all-gather.17.cloned.1.call-update) | async-done | bytes 8388624 | tf_op jit(solution)/shard_map/all_gather | solution.py:27
  151.9 21.5 %select_add_fusion = f32[1024,8192]{1,0:T(8,128)} fusion(f32[1024]{0:T(1024)} %param.10, s32[8192]{0:T(1024)S(1)} %iota_add_fusion, s32[1024]{0:T(1024)S(1)} %iota_add_fusion.1, bf16[512,1024]{1,0:T(8,128)(2,1)S(1)} %bitcast.55, bf16[512,8192]{1,0:T(8,128)(2,1)} %all-gather.17.cloned.1.call-done), kind=kOutput, calls=%fused_computation.2 | convolution fusion | flops 8623489024 | bytes 43032576 | tf_op jit(solution)/shard_map/dot_general | solution.py:28
  173.4 1.9 slice_select_fusion.3
  175.3 0.0 all-gather.19.cloned.1.call-update
  175.3 0.0 all-gather.21.cloned.1.call-start
  175.3 7.3 all-gather.19.cloned.1.call-done
  182.7 1.3 reduce_sum.54
  184.0 0.6 slice_select_fusion.5
  184.6 0.0 all-gather.21.cloned.1.call-update
  184.7 0.0 all-gather.23.cloned.1.call-start
  184.7 4.5 slice_select_fusion.1
  189.3 0.0 all-gather.23.cloned.1.call-update
  189.3 0.3 all-gather.25.cloned.1.call-start
  189.7 52.5 %all-gather.21.cloned.1.call-done = f32[2048,128]{1,0:T(8,128)} async-done(((f32[128,128]{1,0:T(8,128)}), f32[2048,128]{1,0:T(8,128)}) %all-gather.21.cloned.1.call-update) | async-done | bytes 1048592 | tf_op jit(solution)/shard_map/all_gather | solution.py:14
  242.1 1.3 reduce_sum.55
  243.4 0.1 copy.21
  243.5 11.7 cholesky.44
  255.3 0.6 compare_reduce_fusion.1
  255.9 0.7 fusion
  256.6 9.8 custom-call.10
  266.4 0.6 convolution_bitcast_fusion.1
  267.1 644.7 %all-gather.23.cloned.1.call-done = f32[2048,8192]{1,0:T(8,128)} async-done(((f32[128,8192]{1,0:T(8,128)}), f32[2048,8192]{1,0:T(8,128)}) %all-gather.23.cloned.1.call-update) | async-done | bytes 67108880 | tf_op jit(solution)/shard_map/all_gather | solution.py:14
  911.8 23.4 %reduce_sum.56 = f32[128,8192]{1,0:T(8,128)} reduce(f32[16,128,8192]{2,1,0:T(8,128)} %bitcast.10, f32[]{:T(128)} %constant.58.clone.1), dimensions={0}, to_apply=%region_4.7 | reduce | flops 15728640 | bytes 71303168 | tf_op jit(solution)/shard_map/reduce_sum | solution.py:14
  935.2 5.5 fusion.6
  940.6 34.9 %subtract_select_fusion.1 = f32[1024,8192]{1,0:T(8,128)} fusion(f32[1024,8192]{1,0:T(8,128)} %select_add_fusion, pred[8192]{0:T(1024)(128)(4,1)S(1)} %fusion.10, pred[1024]{0:T(1024)(128)(4,1)S(1)} %fusion.12, f32[1024,128]{0,1:T(8,128)S(1)} %convolution_bitcast_fusion.1, f32[128,8192]{1,0:T(8,128)S(1)} %fusion.6), kind=kOutput, calls=%fused_computation.1 | convolution fusion | flops 12910067712 | bytes 71836672 | tf_op jit(solution)/shard_map/dot_general | solution.py:61
  975.5 1.9 slice_select_fusion.2
  977.4 0.0 all-gather.25.cloned.1.call-update
  977.4 0.0 reduce-scatter.2.cloned.1.call-start
  977.5 6.7 fusion.14
  984.2 0.0 reduce-scatter.2.cloned.1.call-update
  984.2 0.0 all-gather.27.cloned.1.call-start
  984.2 0.5 all-gather.25.cloned.1.call-done
  984.8 1.3 reduce_sum.57
  986.1 0.6 slice_select_fusion.4
  986.8 0.0 all-gather.27.cloned.1.call-update
  986.8 0.2 all-gather.29.cloned.1.call-start
  987.0 4.6 slice_select_fusion
  991.6 0.0 all-gather.29.cloned.1.call-update
  991.6 4.2 reduce-scatter.2.cloned.1.call-done
  995.8 1.5 broadcast_multiply_fusion
  997.3 58.1 %all-gather.27.cloned.1.call-done = f32[2048,128]{1,0:T(8,128)} async-done(((f32[128,128]{1,0:T(8,128)}), f32[2048,128]{1,0:T(8,128)}) %all-gather.27.cloned.1.call-update) | async-done | bytes 1048592 | tf_op jit(solution)/shard_map/all_gather | solution.py:14
  1055.3 1.3 reduce_sum.58
  1056.6 0.1 copy.22
  1056.8 11.7 cholesky.55
  1068.5 0.6 compare_reduce_fusion
  1069.1 0.7 fusion.1
  1069.8 9.8 custom-call.12
  1079.6 0.6 convolution_bitcast_fusion
  1080.3 0.1 pad_maximum_fusion
  1080.3 1.3 copy.23
  1081.7 643.6 %all-gather.29.cloned.1.call-done = f32[2048,8192]{1,0:T(8,128)} async-done(((f32[128,8192]{1,0:T(8,128)}), f32[2048,8192]{1,0:T(8,128)}) %all-gather.29.cloned.1.call-update) | async-done | bytes 67108880 | tf_op jit(solution)/shard_map/all_gather | solution.py:14
  1725.2 23.1 %reduce_sum.59 = f32[128,8192]{1,0:T(8,128)} reduce(f32[16,128,8192]{2,1,0:T(8,128)} %bitcast.19, f32[]{:T(128)} %constant.58.clone.1), dimensions={0}, to_apply=%region_7.11 | reduce | flops 15728640 | bytes 71303168 | tf_op jit(solution)/shard_map/reduce_sum | solution.py:14
  1748.3 5.5 fusion.2
  1753.7 34.9 %subtract_select_fusion = f32[1024,8192]{1,0:T(8,128)} fusion(f32[1024,8192]{1,0:T(8,128)} %subtract_select_fusion.1, pred[8192]{0:T(1024)(128)(4,1)S(1)} %fusion.11, pred[1024]{0:T(1024)(128)(4,1)S(1)} %fusion.13, f32[1024,128]{0,1:T(8,128)S(1)} %convolution_bitcast_fusion, f32[128,8192]{1,0:T(8,128)S(1)} %fusion.2), kind=kOutput, calls=%fused_computation | convolution fusion | flops 12910067712 | bytes 71836672 | tf_op jit(solution)/shard_map/dot_general | solution.py:61
  (13 shorter events, 0.2 us)
Async XLA Ops:
  7.2 970.3 %copy-start = (bf16[64,8192]{1,0:T(8,128)(2,1)S(1)}, bf16[64,8192]{1,0:T(8,128)(2,1)}, u32[]{:S(2)}) copy-start(bf16[64,8192]{1,0:T(8,128)(2,1)} %param.9) | copy-start | bytes 3145732
  7.2 14.1 all-gather.15.cloned.1.call-start
  7.9 144.0 %all-gather.17.cloned.1.call-start = ((), (), s32[]{:S(2)}) async-start(), calls=%async_computation.3 | async-start | bytes 8912896 | tf_op jit(solution)/shard_map/all_gather | solution.py:27
  23.6 42.7 %all-to-all-start = ((bf16[32,16,1024]{2,0,1:T(8,128)(2,1)}), bf16[32,16,1024]{2,0,1:T(8,128)(2,1)S(1)}, u32[]{:S(2)}, u32[]{:S(2)}) async-start(bf16[32,16,1024]{2,0,1:T(8,128)(2,1)} %bitcast.54), calls=%async_computation | async-start | bytes 2097152 | tf_op jit(solution)/shard_map/all_to_all | solution.py:26
  30.4 152.2 %all-gather.19.cloned.1.call-start = ((), (), s32[]{:S(2)}) async-start(), calls=%async_computation.5 | async-start | bytes 1572864 | tf_op jit(solution)/shard_map/all_gather | solution.py:14
  175.3 66.8 %all-gather.21.cloned.1.call-start = ((), (), s32[]{:S(2)}) async-start(), calls=%async_computation.6 | async-start | bytes 1114112 | tf_op jit(solution)/shard_map/all_gather | solution.py:14
  184.7 727.1 %all-gather.23.cloned.1.call-start = ((), (), s32[]{:S(2)}) async-start(), calls=%async_computation.7 | async-start | bytes 71303168 | tf_op jit(solution)/shard_map/all_gather | solution.py:14
  189.3 795.5 %all-gather.25.cloned.1.call-start = ((), (), s32[]{:S(2)}) async-start(), calls=%async_computation.8 | async-start | bytes 1572864 | tf_op jit(solution)/shard_map/all_gather | solution.py:14
  977.4 18.4 %reduce-scatter.2.cloned.1.call-start = ((), (), s32[]{:S(2)}) async-start(), calls=%async_computation.4 | async-start | bytes 196608 | tf_op jit(solution)/shard_map/reduce_scatter | solution.py:34
  984.2 71.2 %all-gather.27.cloned.1.call-start = ((), (), s32[]{:S(2)}) async-start(), calls=%async_computation.9 | async-start | bytes 1114112 | tf_op jit(solution)/shard_map/all_gather | solution.py:14
  986.8 738.4 %all-gather.29.cloned.1.call-start = ((), (), s32[]{:S(2)}) async-start(), calls=%async_computation.10 | async-start | bytes 71303168 | tf_op jit(solution)/shard_map/all_gather | solution.py:14
  1753.7 35.0 %copy-start.1 = (bf16[64,8192]{1,0:T(8,128)(2,1)S(1)}, bf16[64,8192]{1,0:T(8,128)(2,1)}, u32[]{:S(2)}) copy-start(bf16[64,8192]{1,0:T(8,128)(2,1)} %param.9) | copy-start | bytes 3145732
Sparse Core Ops, SparseCore 0:
  9.5 11.7 all-gather.14
  24.1 127.8 all-gather.16
  175.4 7.1 all-gather.18
  185.8 56.2 all-gather.20
  244.8 666.9 all-gather.22
  977.5 7.1 all-gather.24
  987.0 8.7 reduce-scatter.1
  999.1 56.1 all-gather.26
  1058.1 667.0 all-gather.28
